TPU v7x, 32 devices: a whole 2x2x4 slice. The times are simulated.
32 devices in a mesh: groups: 2 (over x), expert: 16 (over z, y, core).
Axes of the slice: x: 2, y: 2, z: 4, core: 2. Of those that a mesh axis runs over, the one named last changes fastest.
Arguments:
- queries: bfloat16 [256, 4096], P(('groups', 'expert')), parts along dimension 0, may hold values from -150 to 150
- key_cache: bfloat16 [256, 64, 512], P(('groups', 'expert')), parts along dimension 0, may hold values from -7 to 7
- value_cache: bfloat16 [256, 64, 512], P(('groups', 'expert')), parts along dimension 0, may hold values from -6 to 6
- new_key: bfloat16 [256, 512], P(('groups', 'expert')), parts along dimension 0, may hold values from -6 to 6
- new_value: bfloat16 [256, 512], P(('groups', 'expert')), parts along dimension 0, may hold values from -6 to 6
- cache_lengths: int32 [256], P(('groups', 'expert')), parts along dimension 0, may hold values from 2 to 64, as said below
- hidden_in: bfloat16 [2048, 2048], P(('groups', 'expert')), parts along dimension 0, may hold values from -6 to 6
- norm_gain: bfloat16 [2048], replicated, may hold values from 0.5 to 1.5
- router_weight: bfloat16 [2048, 16], replicated, may hold values from -0.125 to 0.125
- expert_ids: int32 [2048, 8], P(('groups', 'expert')), parts along dimension 0, may hold values from 0 to 15, all different within a row; in each aligned block of 64 rows (0 to 63, 64 to 127, ...) at most 64 rows name the same one
- gate_train: bfloat16 [16, 2048, 768], P(None, 'expert'), may hold values from -0.125 to 0.125
- up_train: bfloat16 [16, 2048, 768], P(None, 'expert'), may hold values from -0.125 to 0.125
- down_train: bfloat16 [16, 768, 2048], P(None, 'expert'), may hold values from -0.21875 to 0.21875
Outputs:
- attended: bfloat16 [256, 4096], P(('groups', 'expert')), parts along dimension 0
- expert_mix: bfloat16 [2048, 2048], P(('groups', 'expert')), parts along dimension 0
There are 2 independent parts, one for each index of `groups`. A program takes and returns all parts, laid end to end along the dimension named above; an argument that names none is the same for every part. Nothing has to cross between parts.
Inputs may be any that keep to these rules, and one draw needn't show every extreme that they name: `expert_ids`: each row names 8 different experts; within the rows of one device no expert is named more than 64 times. `cache_lengths`: the first sequence of each device's 8 has all 64 positions filled.
All inputs are finite; a program needn't handle non-finite values.
Results may differ from a plain program's by a relative error of at most 0.0074.
Values may be sent and summed in bfloat16 or wider, within the bound.
A program may use at most 128 MiB of HBM per device.

v0:
```python
import math
import jax
import jax.numpy as jnp
from jax import lax
from jax.sharding import PartitionSpec as P

HEADS = 32
KV_HEADS = 4
HEAD_DIM = 128
CTX = 64
EPSILON = 1e-06


def rms_normed(hidden_in, norm_gain):
    values = hidden_in.astype(jnp.float32)
    mean_square = jnp.mean(values * values, axis=-1, keepdims=True)
    return (values * lax.rsqrt(mean_square + EPSILON) * norm_gain.astype(jnp.float32)).astype(
        jnp.bfloat16
    )


def attend(queries, key_cache, value_cache, new_key, new_value, cache_lengths):
    seq_count = queries.shape[0]
    group_size = HEADS // KV_HEADS
    query_blocks = queries.reshape(seq_count, KV_HEADS, group_size, HEAD_DIM)
    cached_keys = key_cache.reshape(seq_count, CTX, KV_HEADS, HEAD_DIM)
    cached_values = value_cache.reshape(seq_count, CTX, KV_HEADS, HEAD_DIM)
    fresh_keys = new_key.reshape(seq_count, KV_HEADS, HEAD_DIM)
    fresh_values = new_value.astype(jnp.float32).reshape(seq_count, KV_HEADS, HEAD_DIM)
    score_scale = 1.0 / math.sqrt(HEAD_DIM)
    scores = (
        jnp.einsum("sgrd,scgd->sgrc", query_blocks, cached_keys, preferred_element_type=jnp.float32)
        * score_scale
    )
    own_score = (
        jnp.einsum("sgrd,sgd->sgr", query_blocks, fresh_keys, preferred_element_type=jnp.float32)
        * score_scale
    )
    positions = jnp.arange(CTX, dtype=jnp.int32)
    visible = positions[None, :] < cache_lengths[:, None]
    scores = jnp.where(visible[:, None, None, :], scores, -1e30)
    largest = jnp.maximum(jnp.max(scores, axis=-1), own_score)
    cached_exp = jnp.exp(scores - largest[..., None])
    own_exp = jnp.exp(own_score - largest)
    prob_total = jnp.sum(cached_exp, axis=-1) + own_exp
    cached_prob = (cached_exp / prob_total[..., None]).astype(jnp.bfloat16)
    own_prob = (own_exp / prob_total).astype(jnp.bfloat16).astype(jnp.float32)
    context = jnp.einsum(
        "sgrc,scgd->sgrd", cached_prob, cached_values, preferred_element_type=jnp.float32
    )
    context = context + own_prob[..., None] * fresh_values[:, :, None, :]
    return context.reshape(seq_count, HEADS * HEAD_DIM).astype(jnp.bfloat16)


def expert_rows(received, gate_weight, up_weight, down_weight):
    token_rows = received.reshape(-1, received.shape[2])
    gate_proj = jnp.dot(token_rows, gate_weight, preferred_element_type=jnp.float32)
    up_proj = jnp.dot(token_rows, up_weight, preferred_element_type=jnp.float32)
    hidden_units = (jax.nn.silu(gate_proj) * up_proj).astype(jnp.bfloat16)
    expert_out = jnp.dot(hidden_units, down_weight, preferred_element_type=jnp.float32).astype(
        jnp.bfloat16
    )
    return lax.all_to_all(
        expert_out.reshape(received.shape), "expert", split_axis=0, concat_axis=0, tiled=True
    )


def local(
    queries,
    key_cache,
    value_cache,
    new_key,
    new_value,
    cache_lengths,
    hidden_in,
    norm_gain,
    router_weight,
    expert_ids,
    gate_train,
    up_train,
    down_train,
):
    gate_moved, up_moved, down_moved = (
        lax.all_to_all(gate_train, "expert", split_axis=0, concat_axis=1, tiled=True),
        lax.all_to_all(up_train, "expert", split_axis=0, concat_axis=1, tiled=True),
        lax.all_to_all(down_train, "expert", split_axis=0, concat_axis=1, tiled=True),
    )
    attended = attend(queries, key_cache, value_cache, new_key, new_value, cache_lengths)
    tok_count = hidden_in.shape[0]
    expert_count = router_weight.shape[1]
    top_count = expert_ids.shape[1]
    width = hidden_in.shape[1]
    slot_count = 2 * tok_count * top_count // expert_count
    normed = rms_normed(hidden_in, norm_gain)
    logits = jnp.dot(normed, router_weight, preferred_element_type=jnp.float32)
    expert_range = jnp.arange(expert_count, dtype=jnp.int32)
    picked = expert_ids[:, :, None] == expert_range[None, None, :]
    chosen = jnp.sum(jnp.where(picked, logits[:, None, :], 0.0), axis=-1)
    mixing = jax.nn.softmax(chosen, axis=-1)
    onehot_int = picked.astype(jnp.int32).reshape(-1, expert_count)
    rank_values = jnp.sum((jnp.cumsum(onehot_int, axis=0) - 1) * onehot_int, axis=-1)
    targets = expert_ids.reshape(-1) * slot_count + rank_values
    slot_range = jnp.arange(expert_count * slot_count, dtype=jnp.int32)
    placing = slot_range[:, None] == targets[None, :]
    all_rows, all_ids = (
        lax.all_gather(normed, "expert", axis=0, tiled=True),
        lax.all_gather(expert_ids, "expert", axis=0, tiled=True),
    )
    device_count = lax.axis_size("expert")
    own_index = lax.axis_index("expert")
    own_hits = (all_ids == own_index).astype(jnp.int32).reshape(device_count, tok_count * top_count)
    own_ranks = jnp.cumsum(own_hits, axis=1) - 1
    own_targets = jnp.where(own_hits > 0, own_ranks, -1)
    token_owner = jnp.arange(tok_count * top_count, dtype=jnp.int32) // top_count
    slot_steps = jnp.arange(slot_count, dtype=jnp.int32)
    matches = own_targets[:, None, :] == slot_steps[None, :, None]
    local_token = jnp.sum(jnp.where(matches, token_owner[None, None, :], 0), axis=-1)
    filled = jnp.any(matches, axis=-1)
    row_index = jnp.arange(device_count, dtype=jnp.int32)[:, None] * tok_count + local_token
    taken = jnp.take(all_rows, row_index.reshape(-1), axis=0).reshape(
        device_count, slot_count, width
    )
    received = jnp.where(filled[..., None], taken, jnp.zeros_like(taken))
    returned = expert_rows(received, gate_moved[0], up_moved[0], down_moved[0])
    flat_back = returned.reshape(expert_count * slot_count, width)
    per_assign = lax.dot_general(
        placing.astype(jnp.bfloat16),
        flat_back,
        (((0,), (0,)), ((), ())),
        preferred_element_type=jnp.float32,
    )
    mixed_out = jnp.sum(
        mixing[:, :, None] * per_assign.reshape(tok_count, top_count, width), axis=1
    ).astype(jnp.bfloat16)
    return (attended, mixed_out)


def solution(mesh):
    placed = (
        P(("groups", "expert"), None),
        P(("groups", "expert"), None, None),
        P(("groups", "expert"), None, None),
        P(("groups", "expert"), None),
        P(("groups", "expert"), None),
        P(("groups", "expert")),
        P(("groups", "expert"), None),
        P(),
        P(),
        P(("groups", "expert"), None),
        P(None, "expert", None),
        P(None, "expert", None),
        P(None, "expert", None),
    )
    return jax.shard_map(
        local,
        mesh=mesh,
        in_specs=placed,
        out_specs=(P(("groups", "expert"), None), P(("groups", "expert"), None)),
        check_vma=False,
    )
```

profile of v0, /device:TPU:13, one launch (start us, length us, event | category | flops | bytes accessed | tf_op | source)
XLA Modules:
  0.0 416.2 jit_solution(14784146556622299426)
XLA Ops:
  7.2 0.0 copy-start
  7.2 76.5 %all_to_all.32 = bf16[16,128,768]{2,1,0:T(8,128)(2,1)} all-to-all(bf16[16,128,768]{2,1,0:T(8,128)(2,1)} %param.23), channel_id=1, replica_groups=mesh['groups'=2,'expert'=16] {'expert'}, dimensions={0} | all-to-all | bytes 6291456 | tf_op jit(solution)/shard_map/all_to_all | solution.py:84
  83.7 5.2 %all-to-all-start.1 = ((bf16[16,128,768]{2,1,0:T(8,128)(2,1)}), bf16[16,128,768]{2,1,0:T(8,128)(2,1)}, u32[]{:S(2)}, u32[]{:S(2)}) async-start(bf16[16,128,768]{2,1,0:T(8,128)(2,1)} %param.24), calls=%async_computation.1 | async-start | bytes 6291456 | tf_op jit(solution)/shard_map/all_to_all | solution.py:85
  88.9 0.0 all-gather.3.cloned.1.call-start
  89.0 0.2 fusion.7
  89.2 0.8 fusion.9
  90.0 0.0 all-gather.3.cloned.1.call-update
  90.0 0.0 copy-start.6
  90.0 94.1 %all-to-all-done.1 = bf16[16,128,768]{2,1,0:T(8,128)(2,1)} async-done(((bf16[16,128,768]{2,1,0:T(8,128)(2,1)}), bf16[16,128,768]{2,1,0:T(8,128)(2,1)}, u32[]{:S(2)}, u32[]{:S(2)}) %all-to-all-start.1) | async-done | bytes 3145760 | tf_op jit(solution)/shard_map/all_to_all | solution.py:85
  184.2 4.8 %all-to-all-start.2 = ((bf16[16,48,2048]{2,1,0:T(8,128)(2,1)}), bf16[16,48,2048]{2,1,0:T(8,128)(2,1)}, u32[]{:S(2)}, u32[]{:S(2)}) async-start(bf16[16,48,2048]{2,1,0:T(8,128)(2,1)} %param.25), calls=%async_computation.2 | async-start | bytes 6291456 | tf_op jit(solution)/shard_map/all_to_all | solution.py:86
  189.0 79.5 %all-gather = s32[16,64,8]{1,2,0:T(8,128)S(1)} all-gather(s32[1,64,8]{1,2,0:T(8,128)S(1)} %bitcast.77), channel_id=1, replica_groups=mesh['groups'=2,'expert'=16] {'expert'}, dimensions={0}, use_global_device_ids=true | all-gather | bytes 34816 | tf_op jit(solution)/shard_map/all_gather | solution.py:107
  268.5 0.2 copy.59
  268.7 0.2 copy.60
  268.9 0.1 copy.61
  269.0 1.1 reduce-window.16
  270.1 0.2 slice_reduce_fusion
  270.4 0.1 add_add_fusion
  270.5 0.1 copy.67
  270.6 0.1 copy.64
  270.7 0.4 select_reduce_fusion
  271.1 0.1 broadcast_add_fusion
  271.2 0.1 add.101
  271.3 0.1 add.98
  271.3 0.4 fusion
  271.7 0.1 broadcast_in_dim.86
  271.8 0.0 all-gather.3.cloned.1.call-done
  271.9 11.6 %gather_fusion = bf16[1024,2048]{1,0:T(8,128)(2,1)} fusion(bf16[1024,2048]{1,0:T(8,128)(2,1)} %all-gather.3.cloned.1.call-done, s32[1024]{0:T(1024)S(1)} %broadcast_clamp_fusion), kind=kCustom, calls=%fused_computation | custom fusion | bytes 8392704 | tf_op jit(solution)/shard_map/jit(_take)/gather | solution.py:120
  283.4 8.3 %fusion.32 = f32[1024,768]{1,0:T(8,128)} fusion(bf16[2048,768]{1,0:T(8,128)(2,1)} %bitcast.70, bf16[1024,2048]{1,0:T(8,128)(2,1)} %gather_fusion, pred[1024]{0:T(1024)(128)(4,1)S(1)} %compare_and_fusion, pred[1024]{0:T(1024)(128)(4,1)S(1)} %broadcast_in_dim.86), kind=kOutput, calls=%fused_computation.76 | convolution fusion | flops 3225419776 | bytes 10487808 | tf_op jit(solution)/shard_map/dot_general | solution.py:57
  291.7 13.6 %convolution_convert_fusion = bf16[1024,2048]{1,0:T(8,128)(2,1)} fusion(bf16[768,2048]{1,0:T(8,128)(2,1)} %bitcast.15, f32[1024,768]{1,0:T(8,128)} %fusion.32, bf16[2048,768]{1,0:T(8,128)(2,1)} %bitcast.14, bf16[1024,2048]{1,0:T(8,128)(2,1)} %gather_fusion, pred[1024]{0:T(1024)(128)(4,1)S(1)} %compare_and_fusion, pred[1024]{0:T(1024)(128)(4,1)S(1)} %broadcast_in_dim.86), kind=kOutput, calls=%fused_computation.3 | convolution fusion | flops 6453460992 | bytes 17827840 | tf_op jit(solution)/shard_map/dot_general | solution.py:60
  305.3 0.0 copy-start.9
  305.3 5.1 %all-to-all-start.3 = ((bf16[16,64,2048]{2,1,0:T(8,128)(2,1)}), bf16[16,64,2048]{2,1,0:T(8,128)(2,1)}, u32[]{:S(2)}, u32[]{:S(2)}) async-start(bf16[16,64,2048]{2,1,0:T(8,128)(2,1)} %bitcast.69), calls=%async_computation.3 | async-start | bytes 8388608 | tf_op jit(solution)/shard_map/all_to_all | solution.py:63
  310.4 0.0 copy-start.5
  310.4 0.1 copy.56
  310.5 0.1 reshape.285
  310.6 0.1 eq.78
  310.8 1.2 reduce-window.14
  311.9 0.2 slice_reduce_fusion.1
  312.2 0.1 iota_compare_fusion.5
  312.3 0.2 fusion.17
  312.4 0.5 fusion.33
  312.9 0.2 fusion.14
  313.2 0.3 fusion.5
  313.5 0.7 copy.93
  314.2 0.2 fusion.34
  314.4 0.1 copy.55
  314.5 0.1 fusion.21
  314.6 88.7 %all-to-all-done.3 = bf16[16,64,2048]{2,1,0:T(8,128)(2,1)} async-done(((bf16[16,64,2048]{2,1,0:T(8,128)(2,1)}), bf16[16,64,2048]{2,1,0:T(8,128)(2,1)}, u32[]{:S(2)}, u32[]{:S(2)}) %all-to-all-start.3) | async-done | bytes 4194336 | tf_op jit(solution)/shard_map/all_to_all | solution.py:63
  403.4 6.0 %multiply_reduce_fusion = bf16[64,2048]{1,0:T(8,128)(2,1)} fusion(bf16[1024,2048,1]{1,0,2:T(8,128)(2,1)} %bitcast.18, f32[64,8]{1,0:T(8,128)S(1)} %copy.55, s32[512]{0:T(512)S(1)} %multiply_add_fusion), kind=kOutput, calls=%fused_computation.1 | convolution fusion | flops 2149974016 | bytes 4460544 | tf_op jit(solution)/shard_map/dot_general | solution.py:126
  (42 shorter events, 0.3 us)
Async XLA Ops:
  7.2 306.0 %copy-start = (bf16[8,64,512]{2,1,0:T(8,128)(2,1)S(1)}, bf16[8,64,512]{2,1,0:T(8,128)(2,1)}, u32[]{:S(2)}) copy-start(bf16[8,64,512]{2,1,0:T(8,128)(2,1)} %param.15) | copy-start | bytes 1572868
  83.7 5.3 %copy-start.8 = (bf16[2048]{0:T(1024)(128)(2,1)S(1)}, bf16[2048]{0:T(1024)(128)(2,1)}, u32[]{:S(2)}) copy-start(bf16[2048]{0:T(1024)(128)(2,1)} %param.20) | copy-start | bytes 12292
  83.7 5.3 %copy-start.2 = (bf16[64,2048]{1,0:T(8,128)(2,1)S(1)}, bf16[64,2048]{1,0:T(8,128)(2,1)}, u32[]{:S(2)}) copy-start(bf16[64,2048]{1,0:T(8,128)(2,1)} %param.19) | copy-start | bytes 786436
  83.7 100.5 %all-to-all-start.1 = ((bf16[16,128,768]{2,1,0:T(8,128)(2,1)}), bf16[16,128,768]{2,1,0:T(8,128)(2,1)}, u32[]{:S(2)}, u32[]{:S(2)}) async-start(bf16[16,128,768]{2,1,0:T(8,128)(2,1)} %param.24), calls=%async_computation.1 | async-start | bytes 6291456 | tf_op jit(solution)/shard_map/all_to_all | solution.py:85
  88.9 182.9 %all-gather.3.cloned.1.call-start = ((), (), s32[]{:S(2)}) async-start(), calls=%async_computation.4 | async-start | bytes 4456448 | tf_op jit(solution)/shard_map/all_gather | solution.py:106
  90.0 99.0 %copy-start.6 = (s32[64,8]{0,1:T(8,128)S(1)}, s32[64,8]{0,1:T(8,128)}, u32[]{:S(2)}) copy-start(s32[64,8]{0,1:T(8,128)} %param.22) | copy-start | bytes 6148
  184.2 107.5 %all-to-all-start.2 = ((bf16[16,48,2048]{2,1,0:T(8,128)(2,1)}), bf16[16,48,2048]{2,1,0:T(8,128)(2,1)}, u32[]{:S(2)}, u32[]{:S(2)}) async-start(bf16[16,48,2048]{2,1,0:T(8,128)(2,1)} %param.25), calls=%async_computation.2 | async-start | bytes 6291456 | tf_op jit(solution)/shard_map/all_to_all | solution.py:86
  305.3 5.4 %copy-start.7 = (bf16[8,512]{1,0:T(8,128)(2,1)S(1)}, bf16[8,512]{1,0:T(8,128)(2,1)}, u32[]{:S(2)}) copy-start(bf16[8,512]{1,0:T(8,128)(2,1)} %param.17) | copy-start | bytes 24580
  305.3 6.9 %copy-start.10 = (s32[8]{0:T(128)S(1)}, s32[8]{0:T(128)}, u32[]{:S(2)}) copy-start(s32[8]{0:T(128)} %param.18) | copy-start | bytes 100
  305.3 7.0 %copy-start.4 = (bf16[8,4096]{1,0:T(8,128)(2,1)S(1)}, bf16[8,4096]{1,0:T(8,128)(2,1)}, u32[]{:S(2)}) copy-start(bf16[8,4096]{1,0:T(8,128)(2,1)} %param.13) | copy-start | bytes 196612
  305.3 7.0 %copy-start.9 = (bf16[8,512]{1,0:T(8,128)(2,1)S(1)}, bf16[8,512]{1,0:T(8,128)(2,1)}, u32[]{:S(2)}) copy-start(bf16[8,512]{1,0:T(8,128)(2,1)} %param.16) | copy-start | bytes 24580
  305.3 7.1 %copy-start.3 = (bf16[8,64,512]{2,1,0:T(8,128)(2,1)S(1)}, bf16[8,64,512]{2,1,0:T(8,128)(2,1)}, u32[]{:S(2)}) copy-start(bf16[8,64,512]{2,1,0:T(8,128)(2,1)} %param.14) | copy-start | bytes 1572868
  305.3 98.1 %all-to-all-start.3 = ((bf16[16,64,2048]{2,1,0:T(8,128)(2,1)}), bf16[16,64,2048]{2,1,0:T(8,128)(2,1)}, u32[]{:S(2)}, u32[]{:S(2)}) async-start(bf16[16,64,2048]{2,1,0:T(8,128)(2,1)} %bitcast.69), calls=%async_computation.3 | async-start | bytes 8388608 | tf_op jit(solution)/shard_map/all_to_all | solution.py:63
  310.4 3.7 copy-start.1
  310.4 3.7 copy-start.5
Sparse Core Ops, SparseCore 0:
  92.5 77.4 all-gather.2
where the time goes:
time: 417 us; the launch traced here: 416 us
  waiting for transfers between devices  183 us (44%)
  blocking collectives  156 us (37%)
  matrix products  28.9 us (7%)
  starting transfers between devices  15.2 us (4%)
  between operations  14.3 us (3%)
  local copies, waits for them, and re-layouts  14 us (3%)
  other arithmetic  4.86 us (1%)
    all_to_all x1, waiting for transfers between devices, local(): lax.all_to_all(up_train, 'expert', split_axis=0, concat_axis=1, tiled=True)  94.1 us
    all_to_all x1, waiting for transfers between devices, expert_rows(): lax.all_to_all(expert_out.reshape(received.shape), 'expert', split_axis=0...  88.7 us
    all_gather x1, blocking collectives, local(): lax.all_gather(expert_ids, 'expert', axis=0, tiled=True)  79.5 us
    all_to_all x1, blocking collectives, local(): lax.all_to_all(gate_train, 'expert', split_axis=0, concat_axis=1, tiled=T...  76.5 us
    dot_general x1, matrix products, expert_rows(): jnp.dot(hidden_units, down_weight, preferred_element_type=jnp.float32)  13.6 us
    gather x1, local copies, waits for them, and re-layouts, local(): jnp.take(all_rows, row_index.reshape(-1), axis=0)  11.6 us
  transfers between devices with their start and end apart: 4, of which 2 were waited for; matrix products, arithmetic and copies ran while one was open for 7% of the time, Pallas kernels for 0%

commit v1 on v0

--- a/solution.py
+++ b/solution.py
@@ -104,7 +104,10 @@
     placing = slot_range[:, None] == targets[None, :]
     all_rows, all_ids = (
         lax.all_gather(normed, "expert", axis=0, tiled=True),
-        lax.all_gather(expert_ids, "expert", axis=0, tiled=True),
+        jnp.concatenate(
+            lax.all_to_all(jnp.stack([expert_ids] * lax.axis_size("expert")), "expert", 0, 0),
+            axis=0,
+        ),
     )
     device_count = lax.axis_size("expert")
     own_index = lax.axis_index("expert")

time: 417 us -> 395 us (0.947)
  blocking collectives: 156 us -> 87.2 us
  waiting for transfers between devices: 183 us -> 228 us
    all_gather x1 -> x0, blocking collectives: 79.5 us -> none  [local(): lax.all_gather(expert_ids, 'expert', axis=0, tiled=True)]
    all_to_all x1, waiting for transfers between devices: 0.01 us -> 45.5 us  [local(): lax.all_to_all(down_train, 'expert', split_axis=0, concat_axis=1, tiled=T...]
    all_to_all x0 -> x1, blocking collectives: none -> 10.5 us  [local(): lax.all_to_all(jnp.stack([expert_ids] * lax.axis_size('expert')), 'expert...]
  transfers between devices with their start and end apart: 4 -> 4, of which waited for: 2 -> 3; matrix products, arithmetic and copies ran while one was open for 7% -> 7% of each run, Pallas kernels for 0% -> 0%
where the time goes in v1:
time: 395 us; the launch traced here: 394 us
  waiting for transfers between devices  228 us (58%)
  blocking collectives  87.2 us (22%)
  matrix products  28.9 us (7%)
  local copies, waits for them, and re-layouts  15.4 us (4%)
  starting transfers between devices  14.8 us (4%)
  between operations  14.3 us (4%)
  other arithmetic  5.57 us (1%)
    all_to_all x1, waiting for transfers between devices, local(): lax.all_to_all(up_train, 'expert', split_axis=0, concat_axis=1, tiled=True)  94.1 us
    all_to_all x1, waiting for transfers between devices, expert_rows(): lax.all_to_all(expert_out.reshape(received.shape), 'expert', split_axis=0...  88.2 us
    all_to_all x1, blocking collectives, local(): lax.all_to_all(gate_train, 'expert', split_axis=0, concat_axis=1, tiled=T...  76.7 us
    all_to_all x1, waiting for transfers between devices, local(): lax.all_to_all(down_train, 'expert', split_axis=0, concat_axis=1, tiled=T...  45.5 us
    dot_general x1, matrix products, expert_rows(): jnp.dot(hidden_units, down_weight, preferred_element_type=jnp.float32)  13.6 us
    gather x1, local copies, waits for them, and re-layouts, local(): jnp.take(all_rows, row_index.reshape(-1), axis=0)  11.6 us
    all_to_all x1, blocking collectives, local(): lax.all_to_all(jnp.stack([expert_ids] * lax.axis_size('expert')), 'expert...  10.5 us
    dot_general x1, matrix products, expert_rows(): jnp.dot(token_rows, gate_weight, preferred_element_type=jnp.float32)  8.28 us
  transfers between devices with their start and end apart: 4, of which 3 were waited for; matrix products, arithmetic and copies ran while one was open for 7% of the time, Pallas kernels for 0%

profile of v1, /device:TPU:13, one launch (start us, length us, event | category | flops | bytes accessed | tf_op | source)
XLA Modules:
  0.0 394.1 jit_solution(12866931326653211074)
XLA Ops:
  7.2 0.8 broadcast_bitcast_fusion
  7.9 0.1 reshape.318
  8.0 10.5 %all_to_all.37 = s32[16,1,512]{2,1,0:T(1,128)S(1)} all-to-all(s32[16,1,512]{2,1,0:T(1,128)S(1)} %reshape.318), channel_id=1, replica_groups=mesh['groups'=2,'expert'=16] {'expert'}, dimensions={0} | all-to-all | bytes 65536 | tf_op jit(solution)/shard_map/all_to_all | solution.py:108
  18.5 76.7 %all_to_all.38 = bf16[16,128,768]{2,1,0:T(8,128)(2,1)} all-to-all(bf16[16,128,768]{2,1,0:T(8,128)(2,1)} %param.23), channel_id=1, replica_groups=mesh['groups'=2,'expert'=16] {'expert'}, dimensions={0} | all-to-all | bytes 6291456 | tf_op jit(solution)/shard_map/all_to_all | solution.py:84
  95.2 5.0 %all-to-all-start.2 = ((bf16[16,128,768]{2,1,0:T(8,128)(2,1)}), bf16[16,128,768]{2,1,0:T(8,128)(2,1)}, u32[]{:S(2)}, u32[]{:S(2)}) async-start(bf16[16,128,768]{2,1,0:T(8,128)(2,1)} %param.24), calls=%async_computation.2 | async-start | bytes 6291456 | tf_op jit(solution)/shard_map/all_to_all | solution.py:85
  100.2 0.0 all-gather.2.cloned.1.call-start
  100.3 0.2 fusion.7
  100.5 0.8 fusion.9
  101.3 94.1 %all-to-all-done.2 = bf16[16,128,768]{2,1,0:T(8,128)(2,1)} async-done(((bf16[16,128,768]{2,1,0:T(8,128)(2,1)}), bf16[16,128,768]{2,1,0:T(8,128)(2,1)}, u32[]{:S(2)}, u32[]{:S(2)}) %all-to-all-start.2) | async-done | bytes 3145760 | tf_op jit(solution)/shard_map/all_to_all | solution.py:85
  195.5 4.8 %all-to-all-start.3 = ((bf16[16,48,2048]{2,1,0:T(8,128)(2,1)}), bf16[16,48,2048]{2,1,0:T(8,128)(2,1)}, u32[]{:S(2)}, u32[]{:S(2)}) async-start(bf16[16,48,2048]{2,1,0:T(8,128)(2,1)} %param.25), calls=%async_computation.3 | async-start | bytes 6291456 | tf_op jit(solution)/shard_map/all_to_all | solution.py:86
  200.3 0.5 broadcast.248
  200.8 0.7 reduce.4
  201.5 0.1 reshape.319
  201.6 0.2 copy.59
  201.8 0.2 copy.60
  202.0 0.1 copy.61
  202.1 1.1 reduce-window.16
  203.2 0.2 slice_reduce_fusion
  203.5 0.1 add_add_fusion
  203.6 0.1 copy.67
  203.7 0.1 copy.64
  203.8 0.4 select_reduce_fusion
  204.2 0.1 broadcast_add_fusion
  204.3 0.1 add.101
  204.4 0.1 add.98
  204.4 0.4 fusion
  204.8 0.1 broadcast_in_dim.86
  204.9 11.6 %gather_fusion = bf16[1024,2048]{1,0:T(8,128)(2,1)} fusion(bf16[1024,2048]{1,0:T(8,128)(2,1)} %all-gather.2.cloned.1.call-done, s32[1024]{0:T(1024)S(1)} %broadcast_clamp_fusion), kind=kCustom, calls=%fused_computation | custom fusion | bytes 8392704 | tf_op jit(solution)/shard_map/jit(_take)/gather | solution.py:123
  216.5 8.3 %fusion.32 = f32[1024,768]{1,0:T(8,128)} fusion(bf16[2048,768]{1,0:T(8,128)(2,1)} %bitcast.73, bf16[1024,2048]{1,0:T(8,128)(2,1)} %gather_fusion, pred[1024]{0:T(1024)(128)(4,1)S(1)} %compare_and_fusion, pred[1024]{0:T(1024)(128)(4,1)S(1)} %broadcast_in_dim.86), kind=kOutput, calls=%fused_computation.76 | convolution fusion | flops 3225419776 | bytes 10487808 | tf_op jit(solution)/shard_map/dot_general | solution.py:57
  224.8 45.5 %all-to-all-done.3 = bf16[16,48,2048]{2,1,0:T(8,128)(2,1)} async-done(((bf16[16,48,2048]{2,1,0:T(8,128)(2,1)}), bf16[16,48,2048]{2,1,0:T(8,128)(2,1)}, u32[]{:S(2)}, u32[]{:S(2)}) %all-to-all-start.3) | async-done | bytes 3145760 | tf_op jit(solution)/shard_map/all_to_all | solution.py:86
  270.3 13.6 %convolution_convert_fusion = bf16[1024,2048]{1,0:T(8,128)(2,1)} fusion(bf16[768,2048]{1,0:T(8,128)(2,1)} %bitcast.14, f32[1024,768]{1,0:T(8,128)} %fusion.32, bf16[2048,768]{1,0:T(8,128)(2,1)} %bitcast.13, bf16[1024,2048]{1,0:T(8,128)(2,1)} %gather_fusion, pred[1024]{0:T(1024)(128)(4,1)S(1)} %compare_and_fusion, pred[1024]{0:T(1024)(128)(4,1)S(1)} %broadcast_in_dim.86), kind=kOutput, calls=%fused_computation.3 | convolution fusion | flops 6453460992 | bytes 17827840 | tf_op jit(solution)/shard_map/dot_general | solution.py:60
  283.9 4.9 %all-to-all-start.4 = ((bf16[16,64,2048]{2,1,0:T(8,128)(2,1)}), bf16[16,64,2048]{2,1,0:T(8,128)(2,1)}, u32[]{:S(2)}, u32[]{:S(2)}) async-start(bf16[16,64,2048]{2,1,0:T(8,128)(2,1)} %bitcast.72), calls=%async_computation.4 | async-start | bytes 8388608 | tf_op jit(solution)/shard_map/all_to_all | solution.py:63
  288.8 0.1 copy.56
  288.9 0.1 reshape.298
  289.0 0.1 eq.86
  289.2 1.2 reduce-window.14
  290.3 0.2 slice_reduce_fusion.1
  290.6 0.1 iota_compare_fusion.5
  290.7 0.2 fusion.17
  290.8 0.5 fusion.33
  291.3 0.2 fusion.14
  291.6 0.3 fusion.5
  291.9 0.7 copy.93
  292.6 0.2 fusion.34
  292.8 0.1 copy.55
  292.9 0.1 fusion.21
  293.0 88.2 %all-to-all-done.4 = bf16[16,64,2048]{2,1,0:T(8,128)(2,1)} async-done(((bf16[16,64,2048]{2,1,0:T(8,128)(2,1)}), bf16[16,64,2048]{2,1,0:T(8,128)(2,1)}, u32[]{:S(2)}, u32[]{:S(2)}) %all-to-all-start.4) | async-done | bytes 4194336 | tf_op jit(solution)/shard_map/all_to_all | solution.py:63
  381.3 6.0 %multiply_reduce_fusion = bf16[64,2048]{1,0:T(8,128)(2,1)} fusion(bf16[1024,2048,1]{1,0,2:T(8,128)(2,1)} %bitcast.17, f32[64,8]{1,0:T(8,128)S(1)} %copy.55, s32[512]{0:T(512)S(1)} %multiply_add_fusion), kind=kOutput, calls=%fused_computation.1 | convolution fusion | flops 2149974016 | bytes 4460544 | tf_op jit(solution)/shard_map/dot_general | solution.py:129
  (47 shorter events, 0.4 us)
Async XLA Ops:
  7.2 284.4 %copy-start = (bf16[8,64,512]{2,1,0:T(8,128)(2,1)S(1)}, bf16[8,64,512]{2,1,0:T(8,128)(2,1)}, u32[]{:S(2)}) copy-start(bf16[8,64,512]{2,1,0:T(8,128)(2,1)} %param.15) | copy-start | bytes 1572868
  95.2 5.1 %copy-start.8 = (bf16[2048]{0:T(1024)(128)(2,1)S(1)}, bf16[2048]{0:T(1024)(128)(2,1)}, u32[]{:S(2)}) copy-start(bf16[2048]{0:T(1024)(128)(2,1)} %param.20) | copy-start | bytes 12292
  95.2 5.1 %copy-start.2 = (bf16[64,2048]{1,0:T(8,128)(2,1)S(1)}, bf16[64,2048]{1,0:T(8,128)(2,1)}, u32[]{:S(2)}) copy-start(bf16[64,2048]{1,0:T(8,128)(2,1)} %param.19) | copy-start | bytes 786436
  95.2 100.2 %all-to-all-start.2 = ((bf16[16,128,768]{2,1,0:T(8,128)(2,1)}), bf16[16,128,768]{2,1,0:T(8,128)(2,1)}, u32[]{:S(2)}, u32[]{:S(2)}) async-start(bf16[16,128,768]{2,1,0:T(8,128)(2,1)} %param.24), calls=%async_computation.2 | async-start | bytes 6291456 | tf_op jit(solution)/shard_map/all_to_all | solution.py:85
  100.2 104.7 %all-gather.2.cloned.1.call-start = ((), (), s32[]{:S(2)}) async-start(), calls=%async_computation.5 | async-start | bytes 4456448 | tf_op jit(solution)/shard_map/all_gather | solution.py:106
  195.5 74.8 %all-to-all-start.3 = ((bf16[16,48,2048]{2,1,0:T(8,128)(2,1)}), bf16[16,48,2048]{2,1,0:T(8,128)(2,1)}, u32[]{:S(2)}, u32[]{:S(2)}) async-start(bf16[16,48,2048]{2,1,0:T(8,128)(2,1)} %param.25), calls=%async_computation.3 | async-start | bytes 6291456 | tf_op jit(solution)/shard_map/all_to_all | solution.py:86
  283.8 5.0 %copy-start.6 = (s32[64,8]{0,1:T(8,128)S(1)}, s32[64,8]{0,1:T(8,128)}, u32[]{:S(2)}) copy-start(s32[64,8]{0,1:T(8,128)} %param.22) | copy-start | bytes 6148
  283.8 5.3 %copy-start.7 = (bf16[8,512]{1,0:T(8,128)(2,1)S(1)}, bf16[8,512]{1,0:T(8,128)(2,1)}, u32[]{:S(2)}) copy-start(bf16[8,512]{1,0:T(8,128)(2,1)} %param.17) | copy-start | bytes 24580
  283.9 6.7 %copy-start.10 = (s32[8]{0:T(128)S(1)}, s32[8]{0:T(128)}, u32[]{:S(2)}) copy-start(s32[8]{0:T(128)} %param.18) | copy-start | bytes 100
  283.9 6.8 %copy-start.4 = (bf16[8,4096]{1,0:T(8,128)(2,1)S(1)}, bf16[8,4096]{1,0:T(8,128)(2,1)}, u32[]{:S(2)}) copy-start(bf16[8,4096]{1,0:T(8,128)(2,1)} %param.13) | copy-start | bytes 196612
  283.9 6.8 %copy-start.9 = (bf16[8,512]{1,0:T(8,128)(2,1)S(1)}, bf16[8,512]{1,0:T(8,128)(2,1)}, u32[]{:S(2)}) copy-start(bf16[8,512]{1,0:T(8,128)(2,1)} %param.16) | copy-start | bytes 24580
  283.9 6.9 %copy-start.3 = (bf16[8,64,512]{2,1,0:T(8,128)(2,1)S(1)}, bf16[8,64,512]{2,1,0:T(8,128)(2,1)}, u32[]{:S(2)}) copy-start(bf16[8,64,512]{2,1,0:T(8,128)(2,1)} %param.14) | copy-start | bytes 1572868
  283.9 97.4 %all-to-all-start.4 = ((bf16[16,64,2048]{2,1,0:T(8,128)(2,1)}), bf16[16,64,2048]{2,1,0:T(8,128)(2,1)}, u32[]{:S(2)}, u32[]{:S(2)}) async-start(bf16[16,64,2048]{2,1,0:T(8,128)(2,1)} %bitcast.72), calls=%async_computation.4 | async-start | bytes 8388608 | tf_op jit(solution)/shard_map/all_to_all | solution.py:63
  288.8 3.7 copy-start.1
  288.8 3.7 copy-start.5
Sparse Core Ops, SparseCore 0:
  103.8 77.4 all-gather.1
